TPU v7x, 32 devices: a whole 2x2x4 slice. The times are simulated.
32 devices in a mesh: wide: 16 (over z, y, x), narrow: 2 (over core).
Axes of the slice: x: 2, y: 2, z: 4, core: 2. Of those that a mesh axis runs over, the one named last changes fastest.
Arguments:
- qkv: float32 [3, 2, 1024, 1280], P(None, None, 'wide', 'narrow'), may hold values from -30 to 30
- eta: float32 [2, 1024], P('narrow', 'wide'), may hold values from 0.01 to 0.1
- fast_weights: float32 [2, 640, 3, 384], P('narrow', 'wide'), may hold values from -0.25 to 0.25
- momentum: float32 [2, 640, 3, 384], P('narrow', 'wide'), may hold values from -50 to 50
- ttt_gain: float32 [1280], P('narrow'), may hold values from 0.5 to 1.5
Outputs:
- mixed: float32 [2, 1024, 1280], P(None, 'wide', 'narrow')
- new_weights: float32 [2, 640, 3, 384], P('narrow', 'wide')
- new_momentum: float32 [2, 640, 3, 384], P('narrow', 'wide')
All inputs are finite; a program needn't handle non-finite values.
Results may differ from a plain program's by a relative error of at most 0.0003.
Values sent between devices are 32-bit elements; how exact they have to be, the bound alone decides.
A program may use at most 64 MiB of HBM per device.

v0:
```python
import math
import jax
import jax.numpy as jnp
import numpy as np
from jax import lax
from jax.sharding import PartitionSpec as P

D = 640
ATT = 128
WINDOW = 128
EPSILON = 1e-06
MOMENTUM_RATE = 0.9
STEP_SIZE = 0.03
PRECISION = lax.Precision.HIGHEST


def from_behind(block, axis, distance):
    devices = range(lax.axis_size(axis))
    route = [((i - distance) % len(devices), i) for i in devices]
    return lax.ppermute(block, axis, route)


def product(left, right):
    return jnp.dot(left, right, precision=PRECISION, preferred_element_type=jnp.float32)


def memory_read(inputs, weights):
    gate_pre = product(inputs, weights[:, 0, :])
    up_pre = product(inputs, weights[:, 1, :])
    hidden = jax.nn.silu(gate_pre) * up_pre
    return product(hidden, weights[:, 2, :].T)


def memory_gradient(key_rows, value_rows, rates, weights):
    gate_pre = product(key_rows, weights[:, 0, :])
    up_pre = product(key_rows, weights[:, 1, :])
    sigmoid = jax.nn.sigmoid(gate_pre)
    gated = gate_pre * sigmoid
    hidden = gated * up_pre
    weighted = rates[:, None] * value_rows
    back = -product(weighted, weights[:, 2, :])
    gate_back = back * up_pre * sigmoid * (1.0 + gate_pre * (1.0 - sigmoid))
    up_back = back * gated
    return (weighted, hidden, gate_back, up_back)


def renormalize(weights, moment):
    spread = jnp.sqrt(jnp.mean(moment * moment, axis=0) + EPSILON)
    moved = weights - STEP_SIZE * moment / spread
    ratio = jnp.sqrt(jnp.mean(weights * weights, axis=0) + EPSILON) / jnp.sqrt(
        jnp.mean(moved * moved, axis=0) + EPSILON
    )
    return moved * ratio


def window_attention(query_rows, key_rows, value_rows):
    groups, tok_rows, columns = query_rows.shape
    head_count = columns // ATT
    position = lax.axis_index("wide")
    reach = (WINDOW + tok_rows - 2) // tok_rows
    later_groups = jnp.arange(groups) >= 1
    key_parts, value_parts, offsets, live_parts = ([], [], [], [])
    for back in range(reach, 0, -1):
        keep = min(tok_rows, WINDOW - 1 - (back - 1) * tok_rows)
        got_keys, got_values = from_behind(
            (key_rows[:, tok_rows - keep :], value_rows[:, tok_rows - keep :]), "wide", back
        )
        same_group = position >= back
        key_parts.append(jnp.where(same_group, got_keys, jnp.roll(got_keys, 1, axis=0)))
        value_parts.append(jnp.where(same_group, got_values, jnp.roll(got_values, 1, axis=0)))
        offsets.append(np.arange(keep) + tok_rows - keep - back * tok_rows)
        live_parts.append(
            jnp.broadcast_to(jnp.logical_or(same_group, later_groups)[:, None], (groups, keep))
        )
    key_parts.append(key_rows)
    value_parts.append(value_rows)
    offsets.append(np.arange(tok_rows))
    live_parts.append(jnp.ones((groups, tok_rows), bool))
    near_keys = jnp.concatenate(key_parts, axis=1)
    near_values = jnp.concatenate(value_parts, axis=1)
    live = jnp.concatenate(live_parts, axis=1)
    offset = np.concatenate(offsets)
    distance = np.arange(tok_rows)[:, None] - offset[None, :]
    window_mask = jnp.asarray((distance >= 0) & (distance < WINDOW))
    allowed = live[:, None, None, :] & window_mask[None, None]
    span = near_keys.shape[1]
    queries4 = query_rows.reshape(groups, tok_rows, head_count, ATT)
    keys4 = near_keys.reshape(groups, span, head_count, ATT)
    values4 = near_values.reshape(groups, span, head_count, ATT)
    scores = jnp.einsum("cqhe,ckhe->chqk", queries4, keys4, precision=PRECISION) / math.sqrt(ATT)
    scores = jnp.where(allowed, scores, -1e30)
    highest = jnp.max(scores, axis=-1, keepdims=True)
    weights = jnp.exp(scores - highest)
    weights = weights / jnp.sum(weights, axis=-1, keepdims=True)
    output = jnp.einsum("chqk,ckhe->cqhe", weights, values4, precision=PRECISION)
    return output.reshape(groups, tok_rows, columns)


def local(qkv, eta, fast_weights, momentum, ttt_gain):
    query_rows, key_rows, value_rows = (qkv[0], qkv[1], qkv[2])
    attended = window_attention(query_rows, key_rows, value_rows)
    position = lax.axis_index("wide")
    readouts, updated_list, moment_list = ([], [], [])
    own_weights = fast_weights[0]
    own_moment = momentum[0]
    shard_rows = own_weights.shape[0]
    weights = lax.all_gather(own_weights, "wide", axis=0, tiled=True)
    moment_all = lax.all_gather(own_moment, "wide", axis=0, tiled=True)
    first_keys = key_rows[0, :, 0:D]
    first_values = value_rows[0, :, 0:D]
    first_read = memory_read(query_rows[0, :, 0:D], weights)
    weighted, hidden, gate_back, up_back = memory_gradient(
        first_keys, first_values, eta[0], weights
    )
    total = lax.psum(
        jnp.stack(
            [
                product(first_keys.T, gate_back),
                product(first_keys.T, up_back),
                -product(weighted.T, hidden),
            ],
            axis=1,
        ),
        "wide",
    )
    moment_all = MOMENTUM_RATE * moment_all + total
    updated = renormalize(weights, moment_all)
    new_own = lax.dynamic_slice_in_dim(updated, position * shard_rows, shard_rows, 0)
    new_moment = lax.dynamic_slice_in_dim(moment_all, position * shard_rows, shard_rows, 0)
    second_read = memory_read(query_rows[1, :, 0:D], updated)
    readouts.append(jnp.stack([first_read, second_read]))
    updated_list.append(new_own)
    moment_list.append(new_moment)
    readout = readouts[0]
    squares = lax.psum(jnp.sum(readout * readout, axis=-1), "narrow")
    full_width = readout.shape[-1] * lax.axis_size("narrow")
    scale = jnp.sqrt(squares / full_width + EPSILON)
    mixed = attended + ttt_gain * (readout / scale[..., None])
    return (mixed, jnp.stack(updated_list), jnp.stack(moment_list))


def solution(mesh):
    return jax.shard_map(
        local,
        mesh=mesh,
        in_specs=(
            P(None, None, "wide", "narrow"),
            P("narrow", "wide"),
            P("narrow", "wide", None, None),
            P("narrow", "wide", None, None),
            P("narrow"),
        ),
        out_specs=(
            P(None, "wide", "narrow"),
            P("narrow", "wide", None, None),
            P("narrow", "wide", None, None),
        ),
        check_vma=False,
    )
```

profile of v0, /device:TPU:0, one launch (start us, length us, event | category | flops | bytes accessed | tf_op | source)
XLA Modules:
  0.0 339.0 jit_solution(4695409853012924320)
XLA Ops:
  7.2 1.8 copy.33
  9.1 1.8 copy.35
  10.9 2.1 fusion.63
  13.1 3.0 collective-permute-start.3
  16.0 1.7 slice.112
  17.8 1.5 collective-permute-start.2
  19.3 1.5 collective-permute-start.1
  20.8 1.7 slice.107
  22.5 1.5 collective-permute-start
  27.1 74.0 %all-gather.5.cloned.1.call-done = f32[1,640,3,384]{3,0,2,1:T(1,128)} async-done(((f32[1,40,3,384]{3,0,2,1:T(1,128)}), f32[1,640,3,384]{3,0,2,1:T(1,128)}) %all-gather.5.cloned.1.call-update) | async-done | bytes 2949136 | tf_op jit(solution)/shard_map/all_gather | solution.py:107
  101.1 5.7 %copy.34 = f32[1,640,3,384]{1,3,2,0:T(8,128)S(1)} copy(f32[1,640,3,384]{3,0,2,1:T(1,128)} %all-gather.5.cloned.1.call-done) | data formatting | bytes 5898240 | tf_op jit(solution)/shard_map/all_gather | solution.py:107
  106.8 2.1 fusion.14
  108.9 2.0 fusion.16
  111.0 1.9 fusion
  112.9 1.1 convolution_negate_fusion.1
  116.1 1.8 pad_maximum_fusion
  118.0 1.0 fusion.66
  119.9 1.0 concatenate.45
  121.8 1.0 concatenate.38
  122.9 1.1 fusion.65
  124.0 3.3 fusion.68
  127.7 1.0 fusion.67
  128.7 1.3 convolution_bitcast_fusion.2
  130.1 39.3 %all-gather.7.cloned.1.call-done = f32[1,640,3,384]{3,0,2,1:T(1,128)} async-done(((f32[1,40,3,384]{3,0,2,1:T(1,128)}), f32[1,640,3,384]{3,0,2,1:T(1,128)}) %all-gather.7.cloned.1.call-update) | async-done | bytes 2949136 | tf_op jit(solution)/shard_map/all_gather | solution.py:108
  169.4 7.1 %copy.36 = f32[1,640,3,384]{1,3,2,0:T(8,128)} copy(f32[1,640,3,384]{3,0,2,1:T(1,128)} %all-gather.7.cloned.1.call-done) | data formatting | bytes 5898240 | tf_op jit(solution)/shard_map/all_gather | solution.py:108
  176.5 2.0 fusion.15
  178.5 2.1 convolution_multiply_fusion.1
  181.4 136.0 %all-reduce.2.cloned.1.call-done = f32[640,3,384]{0,2,1:T(8,128)} async-done(((f32[640,3,384]{0,2,1:T(8,128)}), f32[640,3,384]{0,2,1:T(8,128)}) %all-reduce.2.cloned.1.call-update) | async-done | bytes 2949136 | tf_op jit(solution)/shard_map/psum | solution.py:115
  317.3 3.2 multiply_reduce_fusion.2
  322.0 2.1 convolution_bitcast_fusion.6
  324.5 2.1 fusion.3
  327.4 2.5 psum.15
  (56 shorter events, 13.5 us)
Async XLA Ops:
  7.2 16.9 %copy-start.2 = (pred[64,191]{1,0:T(32,128)(4,1)S(1)}, pred[64,191]{1,0:T(32,128)(4,1)}, u32[]{:S(2)}) copy-start(pred[64,191]{1,0:T(32,128)(4,1)} %constant.50.clone) | copy-start | bytes 36676
  7.2 93.9 %all-gather.5.cloned.1.call-start = ((), (), s32[]{:S(2)}) async-start(), calls=%async_computation.1 | async-start | bytes 3133440 | tf_op jit(solution)/shard_map/all_gather | solution.py:107
  9.0 160.4 %all-gather.7.cloned.1.call-start = ((), (), s32[]{:S(2)}) async-start(), calls=%async_computation.2 | async-start | bytes 3133440 | tf_op jit(solution)/shard_map/all_gather | solution.py:108
  10.9 306.4 %all-reduce.2.cloned.1.call-start = ((), (), s32[]{:S(2)}) async-start(), calls=%async_computation | async-start | bytes 5898240 | tf_op jit(solution)/shard_map/psum | solution.py:115
  13.1 109.8 %collective-permute-start.3 = (f32[2,64,640]{2,1,0:T(8,128)}, f32[2,64,640]{2,1,0:T(8,128)}, u32[]{:S(2)}, u32[]{:S(2)}) collective-permute-start(f32[2,64,640]{2,1,0:T(8,128)} %get-tuple-element.9), channel_id=1, source_target_pairs={{30,0},{0,2},{2,4},{4,6},{6,8},{8,10},{10,12},{12,14},{14,16},{16,... | collective-permute-start | bytes 983048 | tf_op jit(solution)/shard_map/ppermute | solution.py:20
  17.8 100.2 %collective-permute-start.2 = (f32[2,63,640]{2,1,0:T(8,128)}, f32[2,63,640]{2,1,0:T(8,128)S(1)}, u32[]{:S(2)}, u32[]{:S(2)}) collective-permute-start(f32[2,63,640]{2,1,0:T(8,128)} %slice.112), channel_id=1, source_target_pairs={{28,0},{30,2},{0,4},{2,6},{4,8},{6,10},{8,12},{10,14},{12,16},{14,... | collective-permute-start | bytes 967688 | tf_op jit(solution)/shard_map/ppermute | solution.py:20
  19.3 108.3 %collective-permute-start.1 = (f32[2,64,640]{2,1,0:T(8,128)}, f32[2,64,640]{2,1,0:T(8,128)}, u32[]{:S(2)}, u32[]{:S(2)}) collective-permute-start(f32[2,64,640]{2,1,0:T(8,128)} %get-tuple-element.8), channel_id=1, source_target_pairs={{30,0},{0,2},{2,4},{4,6},{6,8},{8,10},{10,12},{12,14},{14,16},{16,... | collective-permute-start | bytes 983048 | tf_op jit(solution)/shard_map/ppermute | solution.py:20
  22.5 95.5 %collective-permute-start = (f32[2,63,640]{2,1,0:T(8,128)}, f32[2,63,640]{2,1,0:T(8,128)}, u32[]{:S(2)}, u32[]{:S(2)}) collective-permute-start(f32[2,63,640]{2,1,0:T(8,128)} %slice.107), channel_id=1, source_target_pairs={{28,0},{30,2},{0,4},{2,6},{4,8},{6,10},{8,12},{10,14},{12,16},{14,... | collective-permute-start | bytes 967688 | tf_op jit(solution)/shard_map/ppermute | solution.py:20
  27.1 83.9 %copy-start.4 = (f32[1,64]{1,0:T(1,128)S(1)}, f32[1,64]{1,0:T(1,128)}, u32[]{:S(2)}) copy-start(f32[1,64]{1,0:T(1,128)} %param.7) | copy-start | bytes 772
  106.8 6.1 %copy-start = (f32[3,2,64,640]{3,2,1,0:T(8,128)S(1)}, f32[3,2,64,640]{3,2,1,0:T(8,128)}, u32[]{:S(2)}) copy-start(f32[3,2,64,640]{3,2,1,0:T(8,128)} %param.6) | copy-start | bytes 2949124
  122.9 5.9 %copy-start.1 = (f32[2,64,5,128]{3,1,2,0:T(8,128)S(1)}, f32[2,64,5,128]{3,1,2,0:T(8,128)}, u32[]{:S(2)}) copy-start(f32[2,64,5,128]{3,1,2,0:T(8,128)} %copy.27) | copy-start | bytes 983044
  324.3 7.4 %copy-start.3 = (f32[640]{0:T(1024)S(1)}, f32[640]{0:T(1024)}, u32[]{:S(2)}) copy-start(f32[640]{0:T(1024)} %param.10) | copy-start | bytes 7684
Sparse Core Ops, SparseCore 0:
  11.4 89.6 all-gather.4
  104.4 64.9 all-gather.6
  175.1 142.1 all-reduce.1
where the time goes:
time: 340 us; the launch traced here: 339 us
  waiting for transfers between devices  249 us (73%)
  local copies, waits for them, and re-layouts  33.1 us (10%)
  matrix products  23.6 us (7%)
  between operations  14 us (4%)
  other arithmetic  8.83 us (3%)
  starting transfers between devices  7.62 us (2%)
    psum x1, waiting for transfers between devices, local(): lax.psum(jnp.stack([product(first_keys.T, gate_back), product(first_keys....  136 us
    all_gather x1, waiting for transfers between devices, local(): weights = lax.all_gather(own_weights, 'wide', axis=0, tiled=True)  74 us
    all_gather x1, waiting for transfers between devices, local(): moment_all = lax.all_gather(own_moment, 'wide', axis=0, tiled=True)  39.3 us
    dot_general x12, matrix products, product(): jnp.dot(left, right, precision=PRECISION, preferred_element_type=jnp.floa...  18.9 us
    ppermute x4, starting transfers between devices, from_behind(): return lax.ppermute(block, axis, route)  7.5 us
    all_gather x1, local copies, waits for them, and re-layouts, local(): moment_all = lax.all_gather(own_moment, 'wide', axis=0, tiled=True)  7.07 us
  transfers between devices with their start and end apart: 7, of which 3 were waited for; matrix products, arithmetic and copies ran while one was open for 15% of the time, Pallas kernels for 0%

commit v1 on v0

--- a/solution.py
+++ b/solution.py
@@ -104,8 +104,13 @@
     own_weights = fast_weights[0]
     own_moment = momentum[0]
     shard_rows = own_weights.shape[0]
-    weights = lax.all_gather(own_weights, "wide", axis=0, tiled=True)
-    moment_all = lax.all_gather(own_moment, "wide", axis=0, tiled=True)
+    weights, moment_all = jnp.split(
+        lax.all_gather(
+            jnp.concatenate([own_weights, own_moment], axis=1), "wide", axis=0, tiled=True
+        ),
+        [own_weights.shape[1]],
+        axis=1,
+    )
     first_keys = key_rows[0, :, 0:D]
     first_values = value_rows[0, :, 0:D]
     first_read = memory_read(query_rows[0, :, 0:D], weights)

time: 340 us -> 291 us (0.86)
  waiting for transfers between devices: 249 us -> 204 us
  local copies, waits for them, and re-layouts: 33.1 us -> 23.7 us
  matrix products: 23.6 us -> 27.7 us
    all_gather x2 -> x1, waiting for transfers between devices: 113 us -> 74.8 us  [local(): lax.all_gather(jnp.concatenate([own_weights, own_moment], axis=1), 'wide'...]
    psum x1, waiting for transfers between devices: 136 us -> 113 us  [local(): lax.psum(jnp.stack([product(first_keys.T, gate_back), product(first_keys....]
    ppermute x4, waiting for transfers between devices: 0.01 us -> 15.2 us  [from_behind(): return lax.ppermute(block, axis, route)]
    all_gather x2 -> x0, local copies, waits for them, and re-layouts: 12.8 us -> none  [the longest x1 7.07 us: local(): moment_all = lax.all_gather(own_moment, 'wide', axis=0, tiled=True)]
    unnamed x13 -> x25, local copies, waits for them, and re-layouts: 3.62 us -> 7.89 us
  transfers between devices with their start and end apart: 7 -> 6, of which waited for: 3 -> 3; matrix products, arithmetic and copies ran while one was open for 15% -> 16% of each run, Pallas kernels for 0% -> 0%
where the time goes in v1:
time: 291 us
  waiting for transfers between devices  204 us (70%)
  matrix products  27.7 us (10%)
  local copies, waits for them, and re-layouts  23.7 us (8%)
  between operations  14.4 us (5%)
  other arithmetic  11.2 us (4%)
  starting transfers between devices  7.63 us (3%)
    psum x1, waiting for transfers between devices, local(): lax.psum(jnp.stack([product(first_keys.T, gate_back), product(first_keys....  113 us
    all_gather x1, waiting for transfers between devices, local(): lax.all_gather(jnp.concatenate([own_weights, own_moment], axis=1), 'wide'...  74.8 us
    dot_general x12, matrix products, product(): jnp.dot(left, right, precision=PRECISION, preferred_element_type=jnp.floa...  22.3 us
    ppermute x4, waiting for transfers between devices, from_behind(): return lax.ppermute(block, axis, route)  15.2 us
    unnamed x25, local copies, waits for them, and re-layouts  7.89 us
    ppermute x4, starting transfers between devices, from_behind(): return lax.ppermute(block, axis, route)  7.55 us
  transfers between devices with their start and end apart: 6, of which 3 were waited for; matrix products, arithmetic and copies ran while one was open for 16% of the time, Pallas kernels for 0%

profile of v1, /device:TPU:0, one launch (start us, length us, event | category | flops | bytes accessed | tf_op | source)
XLA Modules:
  0.0 290.6 jit_solution(17954398326398070975)
XLA Ops:
  7.2 1.8 pad_maximum_fusion.1
  9.1 1.3 fusion.62
  10.4 3.0 %collective-permute-start.3 = (f32[2,64,640]{2,1,0:T(8,128)S(1)}, f32[2,64,640]{2,1,0:T(8,128)S(1)}, u32[]{:S(2)}, u32[]{:S(2)}) collective-permute-start(f32[2,64,640]{2,1,0:T(8,128)S(1)} %get-tuple-element.11), channel_id=1, source_target_pairs={{30,0},{0,2},{2,4},{4,6},{6,8},{8,10},{10,12},{12,14},{14,16},{16,... | collective-permute-start | bytes 983048 | tf_op jit(solution)/shard_map/ppermute | solution.py:20
  14.1 1.5 collective-permute-start.2
  15.7 1.5 collective-permute-start.1
  17.9 1.5 collective-permute-start
  22.9 15.2 %collective-permute-done.2 = f32[2,63,640]{2,1,0:T(8,128)} collective-permute-done((f32[2,63,640]{2,1,0:T(8,128)}, f32[2,63,640]{2,1,0:T(8,128)}, u32[]{:S(2)}, u32[]{:S(2)}) %collective-permute-start.2) | collective-permute-done | bytes 322592 | tf_op jit(solution)/shard_map/ppermute | solution.py:20
  38.2 1.0 fusion.63
  39.2 74.8 %all-gather.2.cloned.1.call-done = f32[640,6,384]{2,0,1:T(8,128)} async-done(((f32[40,6,384]{2,0,1:T(8,128)}), f32[640,6,384]{2,0,1:T(8,128)}) %all-gather.2.cloned.1.call-update) | async-done | bytes 5898256 | tf_op jit(solution)/shard_map/all_gather | solution.py:108
  114.0 1.9 convolution_bitcast_fusion.7
  115.9 1.9 convolution_bitcast_fusion.8
  117.9 1.0 fusion
  118.9 1.9 convolution_negate_fusion.1
  120.8 1.0 convolution_bitcast_fusion.1
  122.8 1.8 pad_maximum_fusion
  124.7 1.0 fusion.65
  126.6 1.1 concatenate.41
  128.6 1.1 concatenate.48
  129.9 3.4 %fusion.67 = (f32[2,5,64]{2,1,0:T(8,128)S(1)}, f32[2,5,64,191]{3,2,1,0:T(8,128)S(1)}) fusion(f32[2,64,5,128]{3,2,1,0:T(8,128)} %reshape_squeeze.3, f32[2,64,5,128]{3,1,2,0:T(8,128)} %copy.30, f32[2,64,5,128]{3,1,2,0:T(8,128)S(1)} %copy_bitcast_fusion, f32[2,63,5,128]{3,1,2,0:T(8,128)S(1)} %copy.28, pred[2,64,191]{2,1,0:T(8,128)(4,1)} %broadcast_and_fusion), kind=kOutput, calls=%fused_computation.116 | convolution fusion | flops 188615680 | bytes 1821568 | tf_op jit(solution)/shard_map/cqhe,ckhe->chqk/dot_general | solution.py:90
  133.7 2.0 convolution_bitcast_fusion.2
  135.8 2.9 fusion.61
  138.6 4.7 %copy.40 = f32[640,3,384]{0,2,1:T(8,128)} copy(f32[640,3,384]{2,0,1:T(8,128)} %get-tuple-element.7) | data formatting | bytes 5898240
  143.3 3.1 %copy.39 = f32[640,3,384]{0,2,1:T(8,128)S(1)} copy(f32[640,3,384]{2,0,1:T(8,128)} %get-tuple-element.8) | data formatting | bytes 5898240
  146.5 2.0 convolution_bitcast_fusion.10
  148.4 2.0 fusion.4
  150.4 3.0 %convolution_bitcast_fusion.4 = f32[1,64,640]{2,1,0:T(8,128)} fusion(f32[64,384]{1,0:T(8,128)S(1)} %fusion.4, f32[640,6,384]{2,0,1:T(8,128)} %all-gather.2.cloned.1.call-done), kind=kOutput, calls=%fused_computation.16 | convolution fusion | flops 188743680 | bytes 1245184 | tf_op jit(solution)/shard_map/dot_general | solution.py:24
  153.5 113.5 %all-reduce.2.cloned.1.call-done = f32[640,3,384]{0,2,1:T(8,128)} async-done(((f32[640,3,384]{0,2,1:T(8,128)}), f32[640,3,384]{0,2,1:T(8,128)}) %all-reduce.2.cloned.1.call-update) | async-done | bytes 2949136 | tf_op jit(solution)/shard_map/psum | solution.py:120
  266.9 3.2 %multiply_reduce_fusion.2 = (f32[3,384]{1,0:T(4,128)S(1)}, f32[640,3,384]{0,2,1:T(8,128)S(1)}) fusion(f32[640,3,384]{0,2,1:T(8,128)} %all-reduce.2.cloned.1.call-done, f32[640,3,384]{0,2,1:T(8,128)} %copy.40), kind=kLoop, calls=%fused_computation.4 | loop fusion | flops 2947968 | bytes 8851968 | tf_op jit(solution)/shard_map/reduce_sum | solution.py:48
  271.8 2.2 convolution_bitcast_fusion.6
  275.2 2.3 fusion.3
  277.5 1.9 convolution_bitcast_fusion.3
  280.5 2.5 psum.15
  (66 shorter events, 13.0 us)
Async XLA Ops:
  7.2 12.6 %copy-start.6 = (pred[64,191]{1,0:T(32,128)(4,1)S(1)}, pred[64,191]{1,0:T(32,128)(4,1)}, u32[]{:S(2)}) copy-start(pred[64,191]{1,0:T(32,128)(4,1)} %constant.50.clone) | copy-start | bytes 36676
  7.2 106.8 %all-gather.2.cloned.1.call-start = ((), (), s32[]{:S(2)}) async-start(), calls=%async_computation | async-start | bytes 6266880 | tf_op jit(solution)/shard_map/all_gather | solution.py:108
  9.0 257.9 %all-reduce.2.cloned.1.call-start = ((), (), s32[]{:S(2)}) async-start(), calls=%async_computation.1 | async-start | bytes 5898240 | tf_op jit(solution)/shard_map/psum | solution.py:120
  10.4 119.4 %collective-permute-start.3 = (f32[2,64,640]{2,1,0:T(8,128)S(1)}, f32[2,64,640]{2,1,0:T(8,128)S(1)}, u32[]{:S(2)}, u32[]{:S(2)}) collective-permute-start(f32[2,64,640]{2,1,0:T(8,128)S(1)} %get-tuple-element.11), channel_id=1, source_target_pairs={{30,0},{0,2},{2,4},{4,6},{6,8},{8,10},{10,12},{12,14},{14,16},{16,... | collective-permute-start | bytes 983048 | tf_op jit(solution)/shard_map/ppermute | solution.py:20
  14.1 99.9 %copy-start.1 = (f32[3,2,64,640]{3,2,1,0:T(8,128)S(1)}, f32[3,2,64,640]{3,2,1,0:T(8,128)}, u32[]{:S(2)}) copy-start(f32[3,2,64,640]{3,2,1,0:T(8,128)} %param.6) | copy-start | bytes 2949124
  14.1 24.0 %collective-permute-start.2 = (f32[2,63,640]{2,1,0:T(8,128)}, f32[2,63,640]{2,1,0:T(8,128)}, u32[]{:S(2)}, u32[]{:S(2)}) collective-permute-start(f32[2,63,640]{2,1,0:T(8,128)} %slice.115), channel_id=1, source_target_pairs={{28,0},{30,2},{0,4},{2,6},{4,8},{6,10},{8,12},{10,14},{12,16},{14,... | collective-permute-start | bytes 967688 | tf_op jit(solution)/shard_map/ppermute | solution.py:20
  15.7 117.9 %collective-permute-start.1 = (f32[2,64,640]{2,1,0:T(8,128)S(1)}, f32[2,64,640]{2,1,0:T(8,128)S(1)}, u32[]{:S(2)}, u32[]{:S(2)}) collective-permute-start(f32[2,64,640]{2,1,0:T(8,128)S(1)} %get-tuple-element.10), channel_id=1, source_target_pairs={{30,0},{0,2},{2,4},{4,6},{6,8},{8,10},{10,12},{12,14},{14,16},{16,... | collective-permute-start | bytes 983048 | tf_op jit(solution)/shard_map/ppermute | solution.py:20
  17.9 106.8 %collective-permute-start = (f32[2,63,640]{2,1,0:T(8,128)}, f32[2,63,640]{2,1,0:T(8,128)}, u32[]{:S(2)}, u32[]{:S(2)}) collective-permute-start(f32[2,63,640]{2,1,0:T(8,128)} %slice.110), channel_id=1, source_target_pairs={{28,0},{30,2},{0,4},{2,6},{4,8},{6,10},{8,12},{10,14},{12,16},{14,... | collective-permute-start | bytes 967688 | tf_op jit(solution)/shard_map/ppermute | solution.py:20
  20.6 97.2 %copy-start.8 = (f32[1,64]{1,0:T(1,128)S(1)}, f32[1,64]{1,0:T(1,128)}, u32[]{:S(2)}) copy-start(f32[1,64]{1,0:T(1,128)} %param.7) | copy-start | bytes 772
  126.6 9.1 %slice-start = ((s8[5898240]{0:T(1024)(128)(4,1)}), s8[1703936]{0:T(1024)(128)(4,1)S(1)}, s32[]{:S(2)}) async-start(s8[5898240]{0:T(1024)(128)(4,1)} %bitcast.112), calls=%async_computation.2 | async-start | bytes 3407872
  129.8 3.9 %copy-start.3 = (f32[2,63,5,128]{3,1,2,0:T(8,128)S(1)}, f32[2,63,5,128]{3,1,2,0:T(8,128)}, u32[]{:S(2)}) copy-start(f32[2,63,5,128]{3,1,2,0:T(8,128)} %copy.25) | copy-start | bytes 967684
  129.8 3.9 %copy-start.4 = (f32[2,64,5,128]{3,1,2,0:T(8,128)S(1)}, f32[2,64,5,128]{3,1,2,0:T(8,128)}, u32[]{:S(2)}) copy-start(f32[2,64,5,128]{3,1,2,0:T(8,128)} %copy.27) | copy-start | bytes 983044
  129.9 5.9 %slice-start.1 = ((s8[5898240]{0:T(1024)(128)(4,1)}), s8[4194304]{0:T(1024)(128)(4,1)S(1)}, s32[]{:S(2)}) async-start(s8[5898240]{0:T(1024)(128)(4,1)} %bitcast.112), calls=%async_computation.3 | async-start | bytes 8388608
  271.8 2.3 copy-start
  274.0 6.3 %copy-start.2 = (f32[1,64,640]{2,1,0:T(8,128)S(1)}, f32[1,64,640]{2,1,0:T(8,128)}, u32[]{:S(2)}) copy-start(f32[1,64,640]{2,1,0:T(8,128)} %convolution_bitcast_fusion.4) | copy-start | bytes 491524
  274.1 8.9 %copy-start.5 = (f32[2,5,8,8,128]{4,3,2,1,0:T(8,128)S(1)}, f32[2,5,8,8,128]{4,3,2,1,0:T(8,128)}, u32[]{:S(2)}) copy-start(f32[2,5,8,8,128]{4,3,2,1,0:T(8,128)} %convolution_bitcast_fusion.2) | copy-start | bytes 983044
  274.1 8.9 %copy-start.7 = (f32[640]{0:T(1024)S(1)}, f32[640]{0:T(1024)}, u32[]{:S(2)}) copy-start(f32[640]{0:T(1024)} %param.10) | copy-start | bytes 7684
Sparse Core Ops, SparseCore 0:
  10.7 103.2 all-gather.1
  124.8 142.0 all-reduce.1
